TPU v7x, 32 devices: a whole 2x2x4 slice. The times are simulated.
32 devices in a mesh: dp: 4 (over z), expert: 8 (over y, x, core).
Axes of the slice: x: 2, y: 2, z: 4, core: 2. Of those that a mesh axis runs over, the one named last changes fastest.
Arguments:
- tokens: bfloat16 [2048, 2048], P(('dp', 'expert')), may hold values from -6 to 6
- norm_gain: bfloat16 [2048], replicated, may hold values from 0.099609375 to 1.8984375
- router_weight: bfloat16 [2048, 8], replicated, may hold values from -0.125 to 0.125
- gate_weight: bfloat16 [8, 2048, 5120], P('expert', None, 'dp'), may hold values from -0.125 to 0.125
- up_weight: bfloat16 [8, 2048, 5120], P('expert', None, 'dp'), may hold values from -0.125 to 0.125
- down_weight: bfloat16 [8, 5120, 2048], P('expert', 'dp'), may hold values from -0.078125 to 0.078125
- expert_picks: int32 [4, 8, 128], P('dp'), may hold values from 0 to 511, as said below
- final_gain: bfloat16 [2048], replicated, may hold values from 0.099609375 to 1.8984375
- kv_weight: bfloat16 [2048, 8, 6, 2, 64], P(None, 'expert'), may hold values from -0.125 to 0.125
Outputs:
- moe_out: bfloat16 [2048, 2048], P(('dp', 'expert'))
- kv_cache: bfloat16 [2048, 8, 6, 2, 64], P('dp', 'expert')
Inputs may be any that keep to these rules, and one draw needn't show every extreme that they name: `expert_picks`: for each group and expert, 128 different positions in the group. Of the 64 tokens of one device (positions s * 64 to (s + 1) * 64 - 1) one expert picks at most 32, and for every group and expert some device's tokens are picked exactly 32 times.
All inputs are finite; a program needn't handle non-finite values.
Results may differ from a plain program's by a relative error of at most 0.013.
Values may be sent and summed in bfloat16 or wider, within the bound.
A program may use at most 128 MiB of HBM per device.

v0:
```python
import functools

import jax
import jax.numpy as jnp
from jax import lax
from jax.experimental import pallas as pl
from jax.experimental.pallas import tpu as pltpu
from jax.sharding import PartitionSpec as P

MESH = pl.DeviceIdType.MESH


def normalize(values, gain):
    return (
        values
        * lax.rsqrt(jnp.mean(values * values, axis=-1, keepdims=True) + 1e-06)
        * gain.astype(jnp.float32)
    )


def kernel(
    n, experts, chunks,
    normed, tokens, pick_map, out_map, weight_hi, weight_lo, gate_hbm, up_hbm, down_hbm,
    moe_out, encoded_all,
    gate_w, up_w, down_w, normed_all, gathered, hidden, part, sums, outbound, returned, encoded,
    load_sem, ag_send, ag_recv, z_send, z_recv, rs_send, rs_recv, back_send, back_recv, enc_send, enc_recv,
):
    p = lax.axis_index("dp")
    me = lax.axis_index("expert")
    rows, width = normed.shape
    cap = pick_map.shape[0]
    slots = outbound.shape[0] // experts
    ff = gate_w.shape[1]
    chips = experts // 2
    core = lax.rem(me, 2)
    chip = lax.div(me, 2)
    partner = chip * 2 + (1 - core)

    loads = [
        pltpu.make_async_copy(src.at[0], dst, load_sem.at[i])
        for i, (src, dst) in enumerate(((gate_hbm, gate_w), (up_hbm, up_w), (down_hbm, down_w)))
    ]
    for load in loads:
        load.start()

    barrier = pltpu.get_barrier_semaphore()

    @pl.loop(1, experts)
    def _(k):
        pl.semaphore_signal(barrier, inc=1, device_id={"expert": lax.rem(me + k, experts)}, device_id_type=MESH)

    @pl.when(p > 0)
    def _():
        pl.semaphore_signal(barrier, inc=1, device_id={"dp": p - 1}, device_id_type=MESH)

    @pl.when(p < n - 1)
    def _():
        pl.semaphore_signal(barrier, inc=1, device_id={"dp": p + 1}, device_id_type=MESH)

    neighbours = jnp.where(p > 0, 1, 0) + jnp.where(p < n - 1, 1, 0)
    pl.semaphore_wait(barrier, experts - 1 + neighbours)

    def span(index, size):
        return pl.ds(pl.multiple_of(index * size, size), size)

    tile = width // chunks

    def plane_copy(own, full, send, recv, c, source, target, slot, relay=False):
        cols = span(c, tile)
        place = full.at[span(source, rows), cols]
        return pltpu.make_async_remote_copy(
            src_ref=place if relay else own.at[:, cols],
            dst_ref=place,
            send_sem=send.at[slot, c],
            recv_sem=recv.at[source, c],
            device_id={"expert": target},
            device_id_type=MESH,
        )

    def plane_start(args, c):
        @pl.loop(1, chips)
        def _(k):
            plane_copy(*args, c, me, lax.rem(chip + k, chips) * 2 + core, k).start()

        plane_copy(*args, c, me, partner, 0).start()

    def plane_relay(args, c):
        @pl.loop(1, chips)
        def _(k):
            source = lax.rem(chip + chips - k, chips) * 2 + core
            piece = plane_copy(*args, c, source, partner, chips + k, relay=True)
            piece.wait_recv()
            piece.start()

    def plane_arrive(args, c):
        @pl.loop(0, chips)
        def _(k):
            plane_copy(*args, c, lax.rem(chip + k, chips) * 2 + 1 - core, partner, 0).wait_recv()

    def plane_finish(args, c):
        @pl.loop(0, chips)
        def _(k):
            plane_copy(*args, c, me, partner, k).wait_send()

        @pl.loop(1, chips)
        def _(k):
            plane_copy(*args, c, me, partner, chips + k).wait_send()

    first = (normed, normed_all, ag_send, ag_recv)

    @pl.loop(0, chunks)
    def _(c):
        plane_start(first, c)

    normed_all[span(me, rows)] = normed[...]

    def z_copy(g, c, way, target):
        piece = gathered.at[g, :, span(c, tile)]
        return pltpu.make_async_remote_copy(
            src_ref=piece,
            dst_ref=piece,
            send_sem=z_send.at[way, g, c],
            recv_sem=z_recv.at[g, c],
            device_id={"dp": target},
            device_id_type=MESH,
        )

    def rs_copy(g, c, slot, target):
        return pltpu.make_async_remote_copy(
            src_ref=part.at[g, :, span(c, tile)],
            dst_ref=sums.at[slot, :, span(c, tile)],
            send_sem=rs_send.at[g, c],
            recv_sem=rs_recv.at[slot, c],
            device_id={"dp": target},
            device_id_type=MESH,
        )

    def rs_start(g, c):
        @pl.when(g < p)
        def _():
            rs_copy(g, c, g, p - 1).start()

        @pl.when(g > p)
        def _():
            rs_copy(g, c, jnp.where(g == p + 1, n, g), p + 1).start()

    @pl.loop(0, chunks)
    def _(c):
        plane_relay(first, c)
        plane_arrive(first, c)
        gathered[p, :, span(c, tile)] = jnp.dot(
            pick_map[...], normed_all[:, span(c, tile)], preferred_element_type=jnp.float32
        ).astype(jnp.bfloat16)

        @pl.when(p < n - 1)
        def _():
            z_copy(p, c, 0, p + 1).start()

        @pl.when(p > 0)
        def _():
            z_copy(p, c, 1, p - 1).start()

    for load in loads:
        load.wait()

    ff_tile = 256 if ff % 256 == 0 else 128

    @pl.loop(0, 2 * n - 1)
    def _(j):
        k = lax.div(j + 1, 2)
        odd = lax.rem(j, 2)
        g = p + k * (1 - 2 * odd)

        @pl.when((g >= 0) & (g < n))
        def _():
            @pl.loop(0, chunks)
            def _(c):
                @pl.when(g != p)
                def _():
                    z_copy(g, c, 0, p).wait_recv()

                @pl.when((g < p) & (p < n - 1))
                def _():
                    z_copy(g, c, 0, p + 1).start()

                @pl.when((g > p) & (p > 0))
                def _():
                    z_copy(g, c, 1, p - 1).start()

            @pl.loop(0, ff // ff_tile)
            def _(i):
                cols = span(i, ff_tile)
                block = gathered[g]
                gate = jnp.dot(block, gate_w[:, cols], preferred_element_type=jnp.float32)
                up = jnp.dot(block, up_w[:, cols], preferred_element_type=jnp.float32)
                hidden[:, cols] = (jax.nn.gelu(gate, approximate=True) * up).astype(jnp.bfloat16)

            @pl.loop(0, chunks)
            def _(c):
                cols = span(c, tile)
                part[g, :, cols] = jnp.dot(
                    hidden[...], down_w[:, cols], preferred_element_type=jnp.float32
                ).astype(jnp.bfloat16)

                @pl.when(((g < p) & (p == n - 1)) | ((g > p) & (p == 0)))
                def _():
                    rs_start(g, c)

    left_first = jnp.where(2 * p >= n - 1, 1, 0)

    @pl.loop(0, 2 * (n - 1))
    def _(j):
        is_left = jnp.where(j < n - 1, left_first, 1 - left_first)
        g = p + (1 + lax.rem(j, n - 1)) * (1 - 2 * is_left)
        inner = jnp.where(is_left == 1, (g >= 0) & (p < n - 1), (g < n) & (p > 0))

        @pl.when(inner)
        def _():
            @pl.loop(0, chunks)
            def _(c):
                piece = span(c, tile)
                rs_copy(g, c, g, p).wait_recv()
                part[g, :, piece] = (
                    part[g, :, piece].astype(jnp.float32) + sums[g, :, piece].astype(jnp.float32)
                ).astype(jnp.bfloat16)
                rs_start(g, c)

    def back_copy(c, source, target):
        cols = span(c, tile)
        return pltpu.make_async_remote_copy(
            src_ref=outbound.at[span(target, slots), cols],
            dst_ref=returned.at[span(source, slots), cols],
            send_sem=back_send.at[target, c],
            recv_sem=back_recv.at[source, c],
            device_id={"expert": target},
            device_id_type=MESH,
        )

    second = (encoded, encoded_all, enc_send, enc_recv)

    @pl.loop(0, chunks + 2)
    def _(step):
        @pl.when(step < chunks)
        def _():
            c = step
            cols = span(c, tile)

            @pl.when(p < n - 1)
            def _():
                rs_copy(p, c, p, p).wait_recv()
                part[p, :, cols] = (
                    part[p, :, cols].astype(jnp.float32) + sums[p, :, cols].astype(jnp.float32)
                ).astype(jnp.bfloat16)

            @pl.when(p > 0)
            def _():
                rs_copy(p, c, n, p).wait_recv()
                part[p, :, cols] = (
                    part[p, :, cols].astype(jnp.float32) + sums[n, :, cols].astype(jnp.float32)
                ).astype(jnp.bfloat16)

            outbound[:, cols] = jnp.dot(
                out_map[...], part[p, :, cols], preferred_element_type=jnp.float32
            ).astype(jnp.bfloat16)

            @pl.loop(1, experts)
            def _(k):
                back_copy(c, me, lax.rem(me + k, experts)).start()

            returned[span(me, slots), cols] = outbound[span(me, slots), cols]

        @pl.when((step > 0) & (step <= chunks))
        def _():
            c = step - 1
            cols = span(c, tile)

            @pl.loop(1, experts)
            def _(k):
                back_copy(c, lax.rem(me + k, experts), me).wait_recv()

            block = returned[:, cols]
            value = (
                tokens[:, cols].astype(jnp.float32)
                + jnp.dot(weight_hi[...], block, preferred_element_type=jnp.float32)
                + jnp.dot(weight_lo[...], block, preferred_element_type=jnp.float32)
            ).astype(jnp.bfloat16)
            moe_out[:, cols] = value
            encoded[:, cols] = value
            encoded_all[span(me, rows), cols] = value
            plane_start(second, c)

        @pl.when(step > 1)
        def _():
            plane_relay(second, step - 2)

    @pl.loop(0, chunks)
    def _(c):
        plane_arrive(second, c)

    @pl.loop(0, chunks)
    def _(c):
        plane_finish(first, c)
        plane_finish(second, c)

        @pl.loop(1, experts)
        def _(k):
            back_copy(c, me, lax.rem(me + k, experts)).wait_send()

    @pl.loop(0, n)
    def _(g):
        @pl.loop(0, chunks)
        def _(c):
            @pl.when((g <= p) & (p < n - 1))
            def _():
                z_copy(g, c, 0, p).wait_send()

            @pl.when((g >= p) & (p > 0))
            def _():
                z_copy(g, c, 1, p).wait_send()

            @pl.when(g != p)
            def _():
                rs_copy(g, c, g, p).wait_send()


def kv_kernel(moe_all, gain, weight, out, encoded):
    rows, width = moe_all.shape
    step = 128

    @pl.loop(0, rows // step)
    def _(i):
        piece = pl.ds(pl.multiple_of(i * step, step), step)
        encoded[piece] = normalize(moe_all[piece].astype(jnp.float32), gain[...]).astype(jnp.bfloat16)

    @pl.loop(0, weight.shape[0] // step)
    def _(i):
        piece = pl.ds(pl.multiple_of(i * step, step), step)
        out[piece] = lax.dot_general(
            weight[piece], encoded[...], (((1,), (1,)), ((), ())), preferred_element_type=jnp.float32
        ).astype(jnp.bfloat16)


def local(
    tokens,
    norm_gain,
    router_weight,
    gate_weight,
    up_weight,
    down_weight,
    expert_picks,
    final_gain,
    kv_weight,
):
    n = lax.axis_size("dp")
    experts = lax.axis_size("expert")
    me = lax.axis_index("expert")
    rows, width = tokens.shape
    ff = gate_weight.shape[2]
    chosen = expert_picks[0]
    cap = chosen.shape[1]
    slots = 4 * rows // experts
    wide_tokens = tokens.astype(jnp.float32)
    normed = normalize(wide_tokens, norm_gain).astype(jnp.bfloat16)
    gate_probs = jax.nn.sigmoid(jnp.dot(normed, router_weight, preferred_element_type=jnp.float32))
    source = chosen // rows
    local_row = chosen % rows
    positions = jnp.arange(cap, dtype=jnp.int32)
    earlier = (source[:, :, None] == source[:, None, :]) & (
        positions[None, None, :] < positions[None, :, None]
    )
    slot_rank = jnp.sum(earlier.astype(jnp.int32), axis=2)
    own_chosen = lax.dynamic_index_in_dim(chosen, me, 0, keepdims=False)
    own_rank = lax.dynamic_index_in_dim(slot_rank, me, 0, keepdims=False)
    own_slot = (own_chosen // rows) * slots + own_rank
    pick_map = (own_chosen[:, None] == jnp.arange(experts * rows, dtype=jnp.int32)[None, :]).astype(jnp.bfloat16)
    out_map = (jnp.arange(experts * slots, dtype=jnp.int32)[:, None] == own_slot[None, :]).astype(jnp.bfloat16)
    send_slot = (
        (source == me)[:, :, None] & (slot_rank[:, :, None] == jnp.arange(slots, dtype=jnp.int32))
    ).astype(jnp.bfloat16)
    local_map = (local_row[:, :, None] == jnp.arange(rows, dtype=jnp.int32)).astype(jnp.bfloat16)
    send_map = jnp.einsum("ecm,ect->tem", send_slot, local_map, preferred_element_type=jnp.float32)
    weight = (send_map * gate_probs[:, :, None]).reshape(rows, experts * slots)
    weight_hi = lax.reduce_precision(weight, 8, 7)
    weight_lo = (weight - weight_hi).astype(jnp.bfloat16)
    weight_hi = weight_hi.astype(jnp.bfloat16)

    chunks = 4
    bf16 = jnp.bfloat16
    dma = pltpu.SemaphoreType.DMA
    vmem = pl.BlockSpec(memory_space=pltpu.VMEM)
    hbm = pl.BlockSpec(memory_space=pl.ANY)
    moe_out, moe_all = pl.pallas_call(
        functools.partial(kernel, n, experts, chunks),
        out_shape=(
            jax.ShapeDtypeStruct((rows, width), bf16),
            jax.ShapeDtypeStruct((experts * rows, width), bf16),
        ),
        in_specs=[vmem] * 6 + [hbm] * 3,
        out_specs=(vmem, vmem),
        scratch_shapes=[
            pltpu.VMEM((width, ff), bf16),
            pltpu.VMEM((width, ff), bf16),
            pltpu.VMEM((ff, width), bf16),
            pltpu.VMEM((experts * rows, width), bf16),
            pltpu.VMEM((n, cap, width), bf16),
            pltpu.VMEM((cap, ff), bf16),
            pltpu.VMEM((n, cap, width), bf16),
            pltpu.VMEM((n + 1, cap, width), bf16),
            pltpu.VMEM((experts * slots, width), bf16),
            pltpu.VMEM((experts * slots, width), bf16),
            pltpu.VMEM((rows, width), bf16),
            dma((3,)),
            dma((experts, chunks)),
            dma((experts, chunks)),
            dma((2, n, chunks)),
            dma((n, chunks)),
            dma((n, chunks)),
            dma((n + 1, chunks)),
            dma((experts, chunks)),
            dma((experts, chunks)),
            dma((experts, chunks)),
            dma((experts, chunks)),
        ],
        compiler_params=pltpu.CompilerParams(
            collective_id=0, has_side_effects=True, vmem_limit_bytes=60 * 1024 * 1024
        ),
    )(
        normed, tokens, pick_map, out_map, weight_hi, weight_lo,
        gate_weight, up_weight, down_weight,
    )
    all_rows = moe_all.shape[0]
    kv_matrix = kv_weight.reshape(width, -1).T
    kv_rows = pl.pallas_call(
        kv_kernel,
        out_shape=jax.ShapeDtypeStruct((kv_matrix.shape[0], all_rows), bf16),
        in_specs=[vmem] * 3,
        out_specs=vmem,
        scratch_shapes=[pltpu.VMEM((all_rows, width), bf16)],
        compiler_params=pltpu.CompilerParams(vmem_limit_bytes=40 * 1024 * 1024),
    )(moe_all, final_gain[None, :], kv_matrix)
    kv_cache = kv_rows.T.reshape((all_rows,) + kv_weight.shape[1:])
    return (moe_out, kv_cache)


def solution(mesh):
    in_specs = (
        P(("dp", "expert"), None),
        P(),
        P(),
        P("expert", None, "dp"),
        P("expert", None, "dp"),
        P("expert", "dp", None),
        P("dp", None, None),
        P(),
        P(None, "expert", None, None, None),
    )
    out_specs = (P(("dp", "expert"), None), P("dp", "expert", None, None, None))
    return jax.shard_map(local, mesh=mesh, in_specs=in_specs, out_specs=out_specs, check_vma=False)
```

profile of v0, /device:TPU:0, one launch (start us, length us, event | category | flops | bytes accessed | tf_op | source)
XLA Modules:
  0.0 123.3 jit_solution(3612351678994554258)
XLA Ops:
  0.6 0.0 copy-start
  0.6 1.1 fusion.4
  1.8 0.7 fusion.18
  2.5 0.7 add_select_fusion
  3.2 0.7 broadcast_compare_fusion
  3.9 0.7 convert_element_type.27
  4.6 0.7 broadcast_in_dim.2.gain
  5.3 0.4 convert_reduce_fusion
  5.6 0.7 add_bitcast_fusion
  6.3 0.6 fusion.9.out_map
  7.0 0.7 fusion.7.pick_map
  7.7 1.1 fusion.6.normed
  8.8 0.0 copy-done
  8.8 0.0 copy-start.3
  8.8 0.2 fusion.3
  9.0 0.2 fusion
  9.2 0.1 copy.14
  9.3 0.6 fusion.12
  9.9 0.0 copy-done.3
  10.0 0.0 copy-start.1
  10.0 104.3 %shard_map.104 = (bf16[64,2048]{1,0:T(8,128)(2,1)}, bf16[512,2048]{1,0:T(8,128)(2,1)}) custom-call(bf16[64,2048]{1,0:T(8,128)(2,1)} %copy-done.3, bf16[64,2048]{1,0:T(8,128)(2,1)} %tokens.1, bf16[128,512]{1,0:T(8,128)(2,1)} %fusion.7.pick_map, bf16[256,128]{1,0:T(8,128)(2,1)} %fusion.9.out_map, bf16[64,256]{1,0:T(8,128)(2,1)} %get-tuple-element.9.weight_hi, ...), custom_call_target="tpu_custom_call" | custom-call | tf_op jit(solution)/shard_map/pallas_call | solution.py:392
  114.2 0.0 copy-done.1
  114.2 0.0 copy-start.2
  114.2 1.6 %copy-done.2 = bf16[512,2048]{1,0:T(8,128)(2,1)S(1)} copy-done((bf16[512,2048]{1,0:T(8,128)(2,1)S(1)}, bf16[512,2048]{1,0:T(8,128)(2,1)}, u32[]{:S(2)}) %copy-start.2) | copy-done | bytes 2097176
  115.8 0.0 copy-start.4
  115.8 6.7 %shard_map.105 = bf16[768,512]{1,0:T(8,128)(2,1)} custom-call(bf16[512,2048]{1,0:T(8,128)(2,1)S(1)} %copy-done.2, bf16[1,2048]{1,0:T(2,128)(2,1)S(1)} %broadcast_in_dim.2.gain, bf16[768,2048]{1,0:T(8,128)(2,1)S(1)} %bitcast.54), custom_call_target="tpu_custom_call" | custom-call | tf_op jit(solution)/shard_map/pallas_call | solution.py:433
  122.6 0.0 copy-done.4
  122.6 0.7 copy.17
  (2 shorter events, 0.0 us)
Async XLA Ops:
  0.6 8.2 %copy-start = (bf16[2048,8]{0,1:T(8,128)(2,1)S(1)}, bf16[2048,8]{0,1:T(8,128)(2,1)}, u32[]{:S(2)}) copy-start(bf16[2048,8]{0,1:T(8,128)(2,1)} %param.11) | copy-start | bytes 98308
  8.8 1.1 copy-start.3
  10.0 104.3 %copy-start.1 = (bf16[2048,1,6,2,64]{0,4,3,2,1:T(8,128)(2,1)S(1)}, bf16[2048,1,6,2,64]{0,4,3,2,1:T(8,128)(2,1)}, u32[]{:S(2)}) copy-start(bf16[2048,1,6,2,64]{0,4,3,2,1:T(8,128)(2,1)} %param.17) | copy-start | bytes 9437188
  114.2 1.6 %copy-start.2 = (bf16[512,2048]{1,0:T(8,128)(2,1)S(1)}, bf16[512,2048]{1,0:T(8,128)(2,1)}, u32[]{:S(2)}) copy-start(bf16[512,2048]{1,0:T(8,128)(2,1)} %get-tuple-element.5.moe_all) | copy-start | bytes 6291460
  115.8 6.7 %copy-start.4 = (bf16[64,2048]{1,0:T(8,128)(2,1)S(1)}, bf16[64,2048]{1,0:T(8,128)(2,1)}, u32[]{:S(2)}) copy-start(bf16[64,2048]{1,0:T(8,128)(2,1)} %get-tuple-element.12) | copy-start | bytes 786436
where the time goes:
time: 124 us; the launch traced here: 123 us
  Pallas kernels  111 us (90%)
  other arithmetic  7.38 us (6%)
  local copies, waits for them, and re-layouts  3.8 us (3%)
    pallas_call x1, Pallas kernels, local(): pl.pallas_call(functools.partial(kernel, n, experts, chunks), out_shape=(...  104 us
    pallas_call x1, Pallas kernels, local(): pl.pallas_call(kv_kernel, out_shape=jax.ShapeDtypeStruct((kv_matrix.shape...  6.73 us

commit v1 on v0

v1 whole, which is shorter than its diff:
```python
import functools
import math

import jax
import jax.numpy as jnp
from jax import lax
from jax.experimental import pallas as pl
from jax.experimental.pallas import tpu as pltpu
from jax.sharding import PartitionSpec as P

MESH = pl.DeviceIdType.MESH
F32 = jnp.float32
BF16 = jnp.bfloat16


def plane_slots(side_a, side_b):
    return (side_a - 1) + (side_b - 1) + 1 + (side_a - 1) * (side_b - 1) + side_a * side_b - 1


def kernel(
    n, experts, side_a, side_b, ag_chunks, rs_chunks, lag, keep_map,
    tokens_hbm, gain_hbm, router_hbm, gate_hbm, up_hbm, down_hbm, picks_hbm, final_gain_hbm, kv_hbm,
    moe_out, kv_out,
    gate_w, up_w, down_w, kv_w, tokens_all, gathered, normed, hidden, part, sums, returned,
    gain16, final16, gain, final_gain, router, picks, pick_map, out_map, prob, squares, kv_acc, kv_stage,
    load_sem, ag_send, ag_recv, z_send, z_recv, rs_send, rs_recv, eo_send, eo_recv, out_sem,
):
    p = lax.axis_index("dp")
    me = lax.axis_index("expert")
    cap = picks.shape[1]
    group, width = tokens_all.shape
    rows = group // experts
    ff = gate_w.shape[1]
    heads = kv_acc.shape[0]
    core = lax.rem(me, 2)
    chip = lax.div(me, 2)
    row_at = lax.div(chip, side_b)
    col_at = lax.rem(chip, side_b)
    partner = chip * 2 + (1 - core)

    def span(index, size):
        return pl.ds(pl.multiple_of(index * size, size), size)

    own = span(me, rows)
    loads = [
        pltpu.make_async_copy(src, dst, load_sem.at[i])
        for i, (src, dst) in enumerate((
            (tokens_hbm, tokens_all.at[own]),
            (picks_hbm, picks),
            (gain_hbm, gain16),
            (final_gain_hbm, final16),
            (router_hbm, router),
            (gate_hbm.at[0], gate_w),
            (up_hbm.at[0], up_w),
            (down_hbm.at[0], down_w),
            (kv_hbm, kv_w),
        ))
    ]
    for load in loads:
        load.start()

    def place(a, b):
        return (lax.rem(a + side_a, side_a) * side_b + lax.rem(b + side_b, side_b)) * 2 + core

    square = side_a == side_b

    def peer(i, j, c):
        straight = place(row_at + j, col_at + i)
        if not square:
            return straight
        return jnp.where(lax.rem(c, 2) == 0, straight, place(row_at + i, col_at + j))

    barrier = pltpu.get_barrier_semaphore()

    def greet(target):
        pl.semaphore_signal(barrier, inc=1, device_id={"expert": target}, device_id_type=MESH)

    for i in range(1, side_b):
        greet(place(row_at, col_at + i))
    for j in range(1, side_a):
        greet(place(row_at + j, col_at))
    greet(partner)

    @pl.when(p > 0)
    def _():
        pl.semaphore_signal(barrier, inc=1, device_id={"dp": p - 1}, device_id_type=MESH)

    @pl.when(p < n - 1)
    def _():
        pl.semaphore_signal(barrier, inc=1, device_id={"dp": p + 1}, device_id_type=MESH)

    neighbours = jnp.where(p > 0, 1, 0) + jnp.where(p < n - 1, 1, 0)
    first_peers = range(1, side_b)
    second_peers = range(1, side_a)
    direct = side_a + side_b - 2

    class Plane:
        def __init__(self, full, unit, tile, send, recv):
            self.full, self.unit, self.tile, self.send, self.recv = full, unit, tile, send, recv

        def copy(self, c, source, target, slot):
            where = self.full.at[span(source, self.unit), span(c, self.tile)]
            return pltpu.make_async_remote_copy(
                src_ref=where,
                dst_ref=where,
                send_sem=self.send.at[slot, c],
                recv_sem=self.recv.at[source, c],
                device_id={"expert": target},
                device_id_type=MESH,
            )

        def start(self, c):
            for i in first_peers:
                self.copy(c, me, peer(i, 0, c), i - 1).start()
            for j in second_peers:
                self.copy(c, me, peer(0, j, c), side_b - 1 + j - 1).start()
            self.copy(c, me, partner, direct).start()

        def across(self, c, i, j):
            source = peer(-i, -j, c)
            slot = direct + 1 + (side_a - 1) * (side_b - 1) + i * side_a + j - 1
            piece = self.copy(c, source, partner, slot)
            piece.start()

        def relay(self, c):
            for i in first_peers:
                source = peer(-i, 0, c)
                self.copy(c, source, partner, 0).wait_recv()
                for j in second_peers:
                    slot = direct + 1 + (i - 1) * (side_a - 1) + j - 1
                    self.copy(c, source, peer(0, j, c), slot).start()
                self.across(c, i, 0)

        def collect(self, c):
            for j in second_peers:
                self.copy(c, peer(0, -j, c), partner, 0).wait_recv()
                self.across(c, 0, j)
            for i in first_peers:
                for j in second_peers:
                    self.copy(c, peer(-i, -j, c), partner, 0).wait_recv()
                    self.across(c, i, j)

        def arrive(self, c):
            for i in range(side_b):
                for j in range(side_a):
                    self.copy(c, peer(i, j, c) + 1 - 2 * core, partner, 0).wait_recv()

        def finish(self, c):
            for slot in range(plane_slots(side_a, side_b)):
                self.copy(c, me, partner, slot).wait_send()

    ag_tile = width // ag_chunks
    rs_tile = width // rs_chunks
    first = Plane(tokens_all, rows, ag_tile, ag_send, ag_recv)
    second = Plane(returned, cap, rs_tile, eo_send, eo_recv)

    loads[0].wait()
    pl.semaphore_wait(barrier, direct + 1 + neighbours)

    @pl.loop(0, ag_chunks)
    def _(c):
        first.start(c)

    for load in loads[1:5]:
        load.wait()

    lanes = 128
    for j in range(width // lanes):
        cols = pl.ds(j * lanes, lanes)
        gain[0:1, cols] = gain16[j:j + 1, :].astype(F32)
        final_gain[0:1, cols] = final16[j:j + 1, :].astype(F32)

    chosen = picks[pl.ds(me, 1), :].astype(F32)
    column = jnp.broadcast_to(chosen, (cap, cap)).T
    for j in range(group // cap):
        at = lax.broadcasted_iota(jnp.int32, (cap, cap), 1).astype(F32) + float(j * cap)
        pick_map[:, pl.ds(j * cap, cap)] = jnp.where(column == at, 1.0, 0.0).astype(BF16)

    def z_copy(g, c, way, target):
        piece = gathered.at[g, :, span(c, ag_tile)]
        return pltpu.make_async_remote_copy(
            src_ref=piece,
            dst_ref=piece,
            send_sem=z_send.at[way, g, c],
            recv_sem=z_recv.at[g, c],
            device_id={"dp": target},
            device_id_type=MESH,
        )

    def rs_copy(g, c, slot, target):
        return pltpu.make_async_remote_copy(
            src_ref=part.at[g, :, span(c, rs_tile)],
            dst_ref=sums.at[slot, :, span(c, rs_tile)],
            send_sem=rs_send.at[g, c],
            recv_sem=rs_recv.at[slot, c],
            device_id={"dp": target},
            device_id_type=MESH,
        )

    def rs_start(g, c):
        @pl.when(g < p)
        def _():
            rs_copy(g, c, g, p - 1).start()

        @pl.when(g > p)
        def _():
            rs_copy(g, c, jnp.where(g == p + 1, n, g), p + 1).start()

    @pl.loop(0, ag_chunks + 2)
    def _(s):
        @pl.when(s < ag_chunks)
        def _():
            first.relay(s)

        @pl.when((s >= 1) & (s <= ag_chunks))
        def _():
            first.collect(s - 1)

        @pl.when(s >= 2)
        def _():
            c = s - 2
            cols = span(c, ag_tile)
            first.arrive(c)
            gathered[p, :, cols] = jnp.dot(
                pick_map[...], tokens_all[:, cols], preferred_element_type=F32
            ).astype(BF16)

            @pl.when(p < n - 1)
            def _():
                z_copy(p, c, 0, p + 1).start()

            @pl.when(p > 0)
            def _():
                z_copy(p, c, 1, p - 1).start()

    map_rows = min(group, 256)

    def build_map(i):
        at = lax.broadcasted_iota(jnp.int32, (map_rows, cap), 0) + i * map_rows
        return jnp.concatenate(
            [jnp.where(picks[e:e + 1, :] == at, 1.0, 0.0).astype(BF16) for e in range(experts)], axis=1
        )

    if keep_map:
        @pl.loop(0, group // map_rows)
        def _(i):
            out_map[span(i, map_rows)] = build_map(i)

    kv_acc[...] = jnp.zeros_like(kv_acc)
    squares[...] = jnp.zeros_like(squares)

    @pl.when(p == 0)
    def _():
        sums[n] = jnp.zeros(sums.shape[1:], BF16)

    @pl.when(p == n - 1)
    def _():
        sums[p] = jnp.zeros(sums.shape[1:], BF16)

    for load in loads[5:]:
        load.wait()

    ff_tile = 256 if ff % 256 == 0 else 128
    norm_rows = 32

    def normalize(g):
        @pl.loop(0, cap // norm_rows)
        def _(i):
            piece = span(i, norm_rows)
            value = gathered[g, piece].astype(F32)
            scale = lax.rsqrt(jnp.mean(value * value, axis=-1, keepdims=True) + 1e-06)
            normed[piece] = (value * scale * gain[0:1, :]).astype(BF16)

    def compute(g):
        normalize(g)

        @pl.loop(0, ff // ff_tile)
        def _(i):
            cols = span(i, ff_tile)
            block = normed[...]
            gate = jnp.dot(block, gate_w[:, cols], preferred_element_type=F32)
            up = jnp.dot(block, up_w[:, cols], preferred_element_type=F32)
            hidden[:, cols] = (jax.nn.gelu(gate, approximate=True) * up).astype(BF16)

        @pl.loop(0, rs_chunks)
        def _(c):
            cols = span(c, rs_tile)
            part[g, :, cols] = jnp.dot(
                hidden[...], down_w[:, cols], preferred_element_type=F32
            ).astype(BF16)

            @pl.when(((g < p) & (p == n - 1)) | ((g > p) & (p == 0)))
            def _():
                rs_start(g, c)

    def forward(g, c):
        cols = span(c, rs_tile)
        rs_copy(g, c, g, p).wait_recv()
        part[g, :, cols] = (part[g, :, cols].astype(F32) + sums[g, :, cols].astype(F32)).astype(BF16)
        rs_start(g, c)

    leftmost = jnp.where(2 * p >= n - 1, 1, 0)
    closing = jnp.maximum(p, n - 1 - p)

    def flow(t, s):
        for turn in range(2):
            c = s - turn * lag
            to_left = leftmost if turn == 0 else 1 - leftmost
            g = jnp.where(to_left == 1, n - 1 - t, t)
            live = jnp.where(to_left == 1, (g < p) & (p < n - 1), (g > p) & (p > 0))

            @pl.when(live & (c >= 0) & (c < rs_chunks))
            def _():
                forward(g, c)

    def final(c):
        cols = span(c, rs_tile)

        @pl.when(p < n - 1)
        def _():
            rs_copy(p, c, p, p).wait_recv()

        @pl.when(p > 0)
        def _():
            rs_copy(p, c, n, p).wait_recv()

        value = (
            part[p, :, cols].astype(F32) + sums[p, :, cols].astype(F32) + sums[n, :, cols].astype(F32)
        )
        returned[span(me, cap), cols] = (value * prob[:, 0:1]).astype(BF16)
        second.start(c)

    compute(p)
    logits = lax.dot_general(
        normed[...], router[...], (((1,), (1,)), ((), ())), preferred_element_type=F32
    )
    mine = lax.broadcasted_iota(jnp.int32, logits.shape, 1) == me
    chance = jnp.sum(jnp.where(mine, jax.nn.sigmoid(logits), 0.0), axis=1, keepdims=True)
    prob[...] = jnp.broadcast_to(chance, prob.shape)

    def side_group(t, side):
        return p + t * (2 * side - 1)

    @pl.loop(1, n)
    def _(t):
        @pl.loop(0, ag_chunks)
        def _(c):
            for side in range(2):
                g = side_group(t, side)

                @pl.when((g >= 0) & (g < n))
                def _():
                    z_copy(g, c, 0, p).wait_recv()

                    onward = p + 1 - 2 * side

                    @pl.when((onward >= 0) & (onward < n))
                    def _():
                        z_copy(g, c, side, onward).start()

        @pl.loop(0, 2)
        def _(side):
            g = side_group(t, side)

            @pl.when((g >= 0) & (g < n))
            def _():
                compute(g)

        @pl.when(t < n - 1)
        def _():
            @pl.loop(0, rs_chunks + lag)
            def _(s):
                flow(t, s)

                @pl.when((t == closing) & (s >= lag))
                def _():
                    final(s - lag)

    @pl.loop(0, ag_chunks)
    def _(c):
        first.finish(c)

    def consume(c):
        cols = span(c, rs_tile)
        second.arrive(c)

        @pl.loop(0, group // map_rows)
        def _(i):
            piece = span(i, map_rows)
            chosen_map = out_map[piece] if keep_map else build_map(i)
            value = (
                tokens_all[piece, cols].astype(F32)
                + jnp.dot(chosen_map, returned[:, cols], preferred_element_type=F32)
            ).astype(BF16)
            tokens_all[piece, cols] = value
            wide = value.astype(F32)
            square_sum = wide * wide
            total = square_sum[:, 0:lanes]
            for j in range(1, rs_tile // lanes):
                total = total + square_sum[:, j * lanes:(j + 1) * lanes]
            squares[piece] += total
            scaled = (wide * final_gain[0:1, cols]).astype(BF16)
            kv_acc[:, piece] += lax.dot_general(
                kv_w[:, cols], scaled, (((1,), (1,)), ((), ())), preferred_element_type=F32
            )

    @pl.loop(0, rs_chunks + 3)
    def _(s):
        flow(n - 1, s)

        @pl.when((s < rs_chunks) & (closing == n - 1))
        def _():
            final(s)

        @pl.when((s >= 1) & (s <= rs_chunks))
        def _():
            second.relay(s - 1)

        @pl.when((s >= 2) & (s <= rs_chunks + 1))
        def _():
            second.collect(s - 2)

        @pl.when(s >= 3)
        def _():
            consume(s - 3)

    moe_store = pltpu.make_async_copy(tokens_all.at[own], moe_out, out_sem.at[0])
    moe_store.start()
    mean = jnp.sum(squares[...].T, axis=0, keepdims=True) * (1.0 / width)
    scale = lax.rsqrt(mean + 1e-06)
    out_rows = 128
    stores = []
    for i in range(heads // out_rows):
        piece = pl.ds(i * out_rows, out_rows)
        kv_stage[piece] = (kv_acc[piece] * scale).astype(BF16)
        store = pltpu.make_async_copy(kv_stage.at[piece], kv_out.at[piece], out_sem.at[1 + i])
        store.start()
        stores.append(store)

    @pl.loop(0, rs_chunks)
    def _(c):
        second.finish(c)

    @pl.loop(0, n)
    def _(g):
        @pl.loop(0, ag_chunks)
        def _(c):
            @pl.when((g <= p) & (p < n - 1))
            def _():
                z_copy(g, c, 0, p).wait_send()

            @pl.when((g >= p) & (p > 0))
            def _():
                z_copy(g, c, 1, p).wait_send()

        @pl.when(g != p)
        def _():
            @pl.loop(0, rs_chunks)
            def _(c):
                rs_copy(g, c, g, p).wait_send()

    moe_store.wait()
    for store in stores:
        store.wait()


def local(
    tokens,
    norm_gain,
    router_weight,
    gate_weight,
    up_weight,
    down_weight,
    expert_picks,
    final_gain,
    kv_weight,
):
    n = lax.axis_size("dp")
    experts = lax.axis_size("expert")
    rows, width = tokens.shape
    ff = gate_weight.shape[2]
    cap = expert_picks.shape[2]
    group = experts * rows
    chips = experts // 2
    side_a = max(d for d in range(1, math.isqrt(chips) + 1) if chips % d == 0)
    side_b = chips // side_a
    kv_matrix = kv_weight.reshape(width, -1).T
    heads = kv_matrix.shape[0]
    ag_chunks = 4
    rs_chunks = 4
    lag = 1
    keep_map = group * experts * cap * 2 <= 4 * 1024 * 1024
    dma = pltpu.SemaphoreType.DMA
    slots = plane_slots(side_a, side_b)
    hbm = pl.BlockSpec(memory_space=pl.ANY)
    moe_out, kv_rows = pl.pallas_call(
        functools.partial(kernel, n, experts, side_a, side_b, ag_chunks, rs_chunks, lag, keep_map),
        out_shape=(
            jax.ShapeDtypeStruct((rows, width), BF16),
            jax.ShapeDtypeStruct((heads, group), BF16),
        ),
        in_specs=[hbm] * 9,
        out_specs=(hbm, hbm),
        scratch_shapes=[
            pltpu.VMEM((width, ff), BF16),
            pltpu.VMEM((width, ff), BF16),
            pltpu.VMEM((ff, width), BF16),
            pltpu.VMEM((heads, width), BF16),
            pltpu.VMEM((group, width), BF16),
            pltpu.VMEM((n, cap, width), BF16),
            pltpu.VMEM((cap, width), BF16),
            pltpu.VMEM((cap, ff), BF16),
            pltpu.VMEM((n, cap, width), BF16),
            pltpu.VMEM((n + 1, cap, width), BF16),
            pltpu.VMEM((experts * cap, width), BF16),
            pltpu.VMEM((width // 128, 128), BF16),
            pltpu.VMEM((width // 128, 128), BF16),
            pltpu.VMEM((1, width), F32),
            pltpu.VMEM((1, width), F32),
            pltpu.VMEM((experts, width), BF16),
            pltpu.VMEM((experts, cap), jnp.int32),
            pltpu.VMEM((cap, group), BF16),
            pltpu.VMEM((group, experts * cap) if keep_map else (8, 128), BF16),
            pltpu.VMEM((cap, 128), F32),
            pltpu.VMEM((group, 128), F32),
            pltpu.VMEM((heads, group), F32),
            pltpu.VMEM((heads, group), BF16),
            dma((9,)),
            dma((slots, ag_chunks)),
            dma((experts, ag_chunks)),
            dma((2, n, ag_chunks)),
            dma((n, ag_chunks)),
            dma((n, rs_chunks)),
            dma((n + 1, rs_chunks)),
            dma((slots, rs_chunks)),
            dma((experts, rs_chunks)),
            dma((1 + heads // 128,)),
        ],
        compiler_params=pltpu.CompilerParams(
            collective_id=0, has_side_effects=True, vmem_limit_bytes=67043328
        ),
    )(
        tokens, norm_gain.reshape(-1, 128), router_weight.T, gate_weight, up_weight, down_weight,
        expert_picks[0], final_gain.reshape(-1, 128), kv_matrix,
    )
    kv_cache = kv_rows.T.reshape((group,) + kv_weight.shape[1:])
    return (moe_out, kv_cache)


def solution(mesh):
    in_specs = (
        P(("dp", "expert"), None),
        P(),
        P(),
        P("expert", None, "dp"),
        P("expert", None, "dp"),
        P("expert", "dp", None),
        P("dp", None, None),
        P(),
        P(None, "expert", None, None, None),
    )
    out_specs = (P(("dp", "expert"), None), P("dp", "expert", None, None, None))
    return jax.shard_map(local, mesh=mesh, in_specs=in_specs, out_specs=out_specs, check_vma=False)
```

time: 124 us -> 100 us (0.81)
  Pallas kernels: 111 us -> 95.6 us
  other arithmetic: 7.38 us -> 0 us
    pallas_call x2 -> x1, Pallas kernels: 111 us -> 95.6 us  [local(): pl.pallas_call(functools.partial(kernel, n, experts, side_a, side_b, ag_c...]
    convert_element_type x5 -> x0, other arithmetic: 3.79 us -> none  [the longest x1 1.08 us: local(): normed = normalize(wide_tokens, norm_gain).astype(jnp.bfloat16)]
    reduce_sum x2 -> x0, other arithmetic: 1.47 us -> none  [the longest x1 1.1 us: normalize(): jnp.mean(values * values, axis=-1, keepdims=True) + 1e-06]
    unnamed x11 -> x2, local copies, waits for them, and re-layouts: 2.31 us -> 3.73 us
    eq x2 -> x0, other arithmetic: 1.41 us -> none  [the longest x1 0.71 us: local(): jnp.arange(experts * slots, dtype=jnp.int32)[:, None] == own_slot[None, :]]
where the time goes in v1:
time: 100 us
  Pallas kernels  95.6 us (96%)
  local copies, waits for them, and re-layouts  3.73 us (4%)
    pallas_call x1, Pallas kernels, local(): pl.pallas_call(functools.partial(kernel, n, experts, side_a, side_b, ag_c...  95.6 us
    unnamed x2, local copies, waits for them, and re-layouts  3.73 us

profile of v1, /device:TPU:0, one launch (start us, length us, event | category | flops | bytes accessed | tf_op | source)
XLA Modules:
  0.0 100.0 jit_solution(14971746744065395486)
XLA Ops:
  0.6 95.6 %shard_map.104 = (bf16[64,2048]{1,0:T(8,128)(2,1)}, bf16[768,512]{1,0:T(8,128)(2,1)}) custom-call(bf16[64,2048]{1,0:T(8,128)(2,1)} %tokens_hbm.1, bf16[16,128]{1,0:T(8,128)(2,1)} %bitcast.13, bf16[8,2048]{1,0:T(8,128)(2,1)} %bitcast.12, bf16[1,2048,1280]{2,1,0:T(8,128)(2,1)} %gate_hbm.1, bf16[1,2048,1280]{2,1,0:T(8,128)(2,1)} %up_hbm.1, ...), custom_call_target="tpu_custom_call" | custom-call | tf_op jit(solution)/shard_map/pallas_call | solution.py:496
  96.2 1.7 %copy.13 = bf16[64,2048]{1,0:T(8,128)(2,1)} copy(bf16[64,2048]{1,0:T(8,128)(2,1)} %get-tuple-element.8) | data formatting | bytes 524288
  97.9 2.1 %copy.14 = bf16[512,1,6,2,64]{0,4,3,2,1:T(8,128)(2,1)} copy(bf16[512,1,6,2,64]{0,4,3,2,1:T(8,128)(2,1)} %bitcast.11) | data formatting | bytes 1572864

commit v2 on v1

--- a/solution.py
+++ b/solution.py
@@ -18,10 +18,10 @@
 
 
 def kernel(
-    n, experts, side_a, side_b, ag_chunks, rs_chunks, lag, keep_map,
+    n, experts, side_a, side_b, ag_chunks, rs_chunks, ahead, ag_routed, eo_routed, lag, depth, ff_steps, emit_group, keep_map,
     tokens_hbm, gain_hbm, router_hbm, gate_hbm, up_hbm, down_hbm, picks_hbm, final_gain_hbm, kv_hbm,
     moe_out, kv_out,
-    gate_w, up_w, down_w, kv_w, tokens_all, gathered, normed, hidden, part, sums, returned,
+    gate_w, up_w, down_w, kv_w, tokens_all, gathered, feed, gate_acc, up_acc, row_squares, row_scale, hidden, part, sums, returned,
     gain16, final16, gain, final_gain, router, picks, pick_map, out_map, prob, squares, kv_acc, kv_stage,
     load_sem, ag_send, ag_recv, z_send, z_recv, rs_send, rs_recv, eo_send, eo_recv, out_sem,
 ):
@@ -75,10 +75,12 @@
     def greet(target):
         pl.semaphore_signal(barrier, inc=1, device_id={"expert": target}, device_id_type=MESH)
 
-    for i in range(1, side_b):
-        greet(place(row_at, col_at + i))
-    for j in range(1, side_a):
-        greet(place(row_at + j, col_at))
+    greeted = [
+        (j, i) for j in range(side_a) for i in range(side_b)
+        if (i > 0 or j > 0) and (i == 0 or j == 0 or ag_routed + eo_routed > 0)
+    ]
+    for j, i in greeted:
+        greet(place(row_at + j, col_at + i))
     greet(partner)
 
     @pl.when(p > 0)
@@ -95,8 +97,9 @@
     direct = side_a + side_b - 2
 
     class Plane:
-        def __init__(self, full, unit, tile, send, recv):
+        def __init__(self, full, unit, tile, send, recv, routed):
             self.full, self.unit, self.tile, self.send, self.recv = full, unit, tile, send, recv
+            self.routed = routed
 
         def copy(self, c, source, target, slot):
             where = self.full.at[span(source, self.unit), span(c, self.tile)]
@@ -116,6 +119,12 @@
                 self.copy(c, me, peer(0, j, c), side_b - 1 + j - 1).start()
             self.copy(c, me, partner, direct).start()
 
+            @pl.when(self.routed(c))
+            def _():
+                for i in first_peers:
+                    for j in second_peers:
+                        self.copy(c, me, peer(i, j, c), direct + 1 + (i - 1) * (side_a - 1) + j - 1).start()
+
         def across(self, c, i, j):
             source = peer(-i, -j, c)
             slot = direct + 1 + (side_a - 1) * (side_b - 1) + i * side_a + j - 1
@@ -126,9 +135,13 @@
             for i in first_peers:
                 source = peer(-i, 0, c)
                 self.copy(c, source, partner, 0).wait_recv()
-                for j in second_peers:
-                    slot = direct + 1 + (i - 1) * (side_a - 1) + j - 1
-                    self.copy(c, source, peer(0, j, c), slot).start()
+
+                @pl.when(jnp.logical_not(self.routed(c)))
+                def _():
+                    for j in second_peers:
+                        slot = direct + 1 + (i - 1) * (side_a - 1) + j - 1
+                        self.copy(c, source, peer(0, j, c), slot).start()
+
                 self.across(c, i, 0)
 
         def collect(self, c):
@@ -151,14 +164,13 @@
 
     ag_tile = width // ag_chunks
     rs_tile = width // rs_chunks
-    first = Plane(tokens_all, rows, ag_tile, ag_send, ag_recv)
-    second = Plane(returned, cap, rs_tile, eo_send, eo_recv)
+    first = Plane(tokens_all, rows, ag_tile, ag_send, ag_recv, lambda c: c < ag_routed)
+    second = Plane(returned, cap, rs_tile, eo_send, eo_recv, lambda c: c >= rs_chunks - eo_routed)
 
     loads[0].wait()
-    pl.semaphore_wait(barrier, direct + 1 + neighbours)
-
-    @pl.loop(0, ag_chunks)
-    def _(c):
+    pl.semaphore_wait(barrier, len(greeted) + 1 + neighbours)
+
+    for c in range(min(ahead, ag_chunks)):
         first.start(c)
 
     for load in loads[1:5]:
@@ -212,6 +224,10 @@
         def _():
             first.relay(s)
 
+        @pl.when(s + ahead < ag_chunks)
+        def _():
+            first.start(s + ahead)
+
         @pl.when((s >= 1) & (s <= ag_chunks))
         def _():
             first.collect(s - 1)
@@ -233,7 +249,7 @@
             def _():
                 z_copy(p, c, 1, p - 1).start()
 
-    map_rows = min(group, 256)
+    map_rows = min(group, 512) if keep_map else 256
 
     def build_map(i):
         at = lax.broadcasted_iota(jnp.int32, (map_rows, cap), 0) + i * map_rows
@@ -260,38 +276,56 @@
     for load in loads[5:]:
         load.wait()
 
-    ff_tile = 256 if ff % 256 == 0 else 128
-    norm_rows = 32
-
-    def normalize(g):
-        @pl.loop(0, cap // norm_rows)
-        def _(i):
-            piece = span(i, norm_rows)
-            value = gathered[g, piece].astype(F32)
-            scale = lax.rsqrt(jnp.mean(value * value, axis=-1, keepdims=True) + 1e-06)
-            normed[piece] = (value * scale * gain[0:1, :]).astype(BF16)
-
-    def compute(g):
-        normalize(g)
+    ff_tile = ff // ff_steps
+
+    def absorb(g, c, slot):
+        cols = pl.ds(c * ag_tile, ag_tile)
+        value = gathered[g, :, cols].astype(F32)
+        squared = value * value
+        total = squared[:, 0:lanes]
+        for j in range(1, ag_tile // lanes):
+            total = total + squared[:, j * lanes:(j + 1) * lanes]
+        if c > 0:
+            total = total + row_squares[slot]
+        row_squares[slot] = total
+        feed[...] = (value * gain[0:1, cols]).astype(BF16)
+        closes = c == ag_chunks - 1
+        if closes:
+            row_scale[slot] = jnp.broadcast_to(
+                lax.rsqrt(jnp.sum(total, axis=1, keepdims=True) * (1.0 / width) + 1e-06), total.shape
+            )
 
         @pl.loop(0, ff // ff_tile)
         def _(i):
-            cols = span(i, ff_tile)
-            block = normed[...]
-            gate = jnp.dot(block, gate_w[:, cols], preferred_element_type=F32)
-            up = jnp.dot(block, up_w[:, cols], preferred_element_type=F32)
-            hidden[:, cols] = (jax.nn.gelu(gate, approximate=True) * up).astype(BF16)
-
-        @pl.loop(0, rs_chunks)
-        def _(c):
-            cols = span(c, rs_tile)
+            tile = span(i, ff_tile)
+            block = feed[...]
+            gate = jnp.dot(block, gate_w[cols, tile], preferred_element_type=F32)
+            up = jnp.dot(block, up_w[cols, tile], preferred_element_type=F32)
+            if c > 0:
+                gate = gate + gate_acc[slot, :, tile]
+                up = up + up_acc[slot, :, tile]
+            if closes:
+                scale = row_scale[slot, :, 0:1]
+                hidden[:, tile] = (jax.nn.gelu(gate * scale, approximate=True) * (up * scale)).astype(BF16)
+            else:
+                gate_acc[slot, :, tile] = gate
+                up_acc[slot, :, tile] = up
+
+    def emit(g):
+        leads = ((g < p) & (p == n - 1)) | ((g > p) & (p == 0))
+        wide = rs_tile * emit_group
+
+        @pl.loop(0, rs_chunks // emit_group)
+        def _(i):
+            cols = span(i, wide)
             part[g, :, cols] = jnp.dot(
                 hidden[...], down_w[:, cols], preferred_element_type=F32
             ).astype(BF16)
 
-            @pl.when(((g < p) & (p == n - 1)) | ((g > p) & (p == 0)))
+            @pl.when(leads)
             def _():
-                rs_start(g, c)
+                for j in range(emit_group):
+                    rs_start(g, i * emit_group + j)
 
     def forward(g, c):
         cols = span(c, rs_tile)
@@ -327,13 +361,18 @@
         value = (
             part[p, :, cols].astype(F32) + sums[p, :, cols].astype(F32) + sums[n, :, cols].astype(F32)
         )
+
         returned[span(me, cap), cols] = (value * prob[:, 0:1]).astype(BF16)
         second.start(c)
 
-    compute(p)
-    logits = lax.dot_general(
-        normed[...], router[...], (((1,), (1,)), ((), ())), preferred_element_type=F32
-    )
+    logits = jnp.zeros((cap, experts), F32)
+    for c in range(ag_chunks):
+        absorb(p, c, 0)
+        logits = logits + lax.dot_general(
+            feed[...], router[:, pl.ds(c * ag_tile, ag_tile)], (((1,), (1,)), ((), ())), preferred_element_type=F32
+        )
+    emit(p)
+    logits = logits * row_scale[0, :, 0:1]
     mine = lax.broadcasted_iota(jnp.int32, logits.shape, 1) == me
     chance = jnp.sum(jnp.where(mine, jax.nn.sigmoid(logits), 0.0), axis=1, keepdims=True)
     prob[...] = jnp.broadcast_to(chance, prob.shape)
@@ -343,28 +382,22 @@
 
     @pl.loop(1, n)
     def _(t):
-        @pl.loop(0, ag_chunks)
-        def _(c):
+        for c in range(ag_chunks):
             for side in range(2):
                 g = side_group(t, side)
 
                 @pl.when((g >= 0) & (g < n))
                 def _():
                     z_copy(g, c, 0, p).wait_recv()
-
                     onward = p + 1 - 2 * side
 
                     @pl.when((onward >= 0) & (onward < n))
                     def _():
                         z_copy(g, c, side, onward).start()
 
-        @pl.loop(0, 2)
-        def _(side):
-            g = side_group(t, side)
-
-            @pl.when((g >= 0) & (g < n))
-            def _():
-                compute(g)
+                    absorb(g, c, side)
+                    if c == ag_chunks - 1:
+                        emit(g)
 
         @pl.when(t < n - 1)
         def _():
@@ -404,7 +437,7 @@
                 kv_w[:, cols], scaled, (((1,), (1,)), ((), ())), preferred_element_type=F32
             )
 
-    @pl.loop(0, rs_chunks + 3)
+    @pl.loop(0, rs_chunks + 3 * depth)
     def _(s):
         flow(n - 1, s)
 
@@ -412,17 +445,17 @@
         def _():
             final(s)
 
-        @pl.when((s >= 1) & (s <= rs_chunks))
-        def _():
-            second.relay(s - 1)
-
-        @pl.when((s >= 2) & (s <= rs_chunks + 1))
-        def _():
-            second.collect(s - 2)
-
-        @pl.when(s >= 3)
-        def _():
-            consume(s - 3)
+        @pl.when((s >= depth) & (s < rs_chunks + depth))
+        def _():
+            second.relay(s - depth)
+
+        @pl.when((s >= 2 * depth) & (s < rs_chunks + 2 * depth))
+        def _():
+            second.collect(s - 2 * depth)
+
+        @pl.when(s >= 3 * depth)
+        def _():
+            consume(s - 3 * depth)
 
     moe_store = pltpu.make_async_copy(tokens_all.at[own], moe_out, out_sem.at[0])
     moe_store.start()
@@ -487,14 +520,20 @@
     kv_matrix = kv_weight.reshape(width, -1).T
     heads = kv_matrix.shape[0]
     ag_chunks = 4
-    rs_chunks = 4
-    lag = 1
+    rs_chunks = 8
+    ahead = 2
+    ag_routed = 0
+    eo_routed = 0
+    lag = 2
+    depth = 2
+    ff_steps = 1
+    emit_group = 4
     keep_map = group * experts * cap * 2 <= 4 * 1024 * 1024
     dma = pltpu.SemaphoreType.DMA
     slots = plane_slots(side_a, side_b)
     hbm = pl.BlockSpec(memory_space=pl.ANY)
     moe_out, kv_rows = pl.pallas_call(
-        functools.partial(kernel, n, experts, side_a, side_b, ag_chunks, rs_chunks, lag, keep_map),
+        functools.partial(kernel, n, experts, side_a, side_b, ag_chunks, rs_chunks, ahead, ag_routed, eo_routed, lag, depth, ff_steps, emit_group, keep_map),
         out_shape=(
             jax.ShapeDtypeStruct((rows, width), BF16),
             jax.ShapeDtypeStruct((heads, group), BF16),
@@ -508,7 +547,11 @@
             pltpu.VMEM((heads, width), BF16),
             pltpu.VMEM((group, width), BF16),
             pltpu.VMEM((n, cap, width), BF16),
-            pltpu.VMEM((cap, width), BF16),
+            pltpu.VMEM((cap, width // ag_chunks), BF16),
+            pltpu.VMEM((2, cap, ff), F32),
+            pltpu.VMEM((2, cap, ff), F32),
+            pltpu.VMEM((2, cap, 128), F32),
+            pltpu.VMEM((2, cap, 128), F32),
             pltpu.VMEM((cap, ff), BF16),
             pltpu.VMEM((n, cap, width), BF16),
             pltpu.VMEM((n + 1, cap, width), BF16),

time: 100 us -> 95.1 us (0.951)
  Pallas kernels: 95.6 us -> 90.5 us
    pallas_call x1, Pallas kernels: 95.6 us -> 90.5 us  [local(): pl.pallas_call(functools.partial(kernel, n, experts, side_a, side_b, ag_c...]
where the time goes in v2:
time: 95.1 us; the launch traced here: 94.9 us
  Pallas kernels  90.5 us (95%)
  local copies, waits for them, and re-layouts  3.73 us (4%)
    pallas_call x1, Pallas kernels, local(): pl.pallas_call(functools.partial(kernel, n, experts, side_a, side_b, ag_c...  90.5 us
    unnamed x2, local copies, waits for them, and re-layouts  3.73 us

profile of v2, /device:TPU:0, one launch (start us, length us, event | category | flops | bytes accessed | tf_op | source)
XLA Modules:
  0.0 94.9 jit_solution(17626880063406121148)
XLA Ops:
  0.6 90.5 %shard_map.104 = (bf16[64,2048]{1,0:T(8,128)(2,1)}, bf16[768,512]{1,0:T(8,128)(2,1)}) custom-call(bf16[64,2048]{1,0:T(8,128)(2,1)} %tokens_hbm.1, bf16[16,128]{1,0:T(8,128)(2,1)} %bitcast.13, bf16[8,2048]{1,0:T(8,128)(2,1)} %bitcast.12, bf16[1,2048,1280]{2,1,0:T(8,128)(2,1)} %gate_hbm.1, bf16[1,2048,1280]{2,1,0:T(8,128)(2,1)} %up_hbm.1, ...), custom_call_target="tpu_custom_call" | custom-call | tf_op jit(solution)/shard_map/pallas_call | solution.py:535
  91.2 1.7 %copy.13 = bf16[64,2048]{1,0:T(8,128)(2,1)} copy(bf16[64,2048]{1,0:T(8,128)(2,1)} %get-tuple-element.8) | data formatting | bytes 524288
  92.8 2.1 %copy.14 = bf16[512,1,6,2,64]{0,4,3,2,1:T(8,128)(2,1)} copy(bf16[512,1,6,2,64]{0,4,3,2,1:T(8,128)(2,1)} %bitcast.11) | data formatting | bytes 1572864

commit v3 on v2

--- a/solution.py
+++ b/solution.py
@@ -188,6 +188,13 @@
         at = lax.broadcasted_iota(jnp.int32, (cap, cap), 1).astype(F32) + float(j * cap)
         pick_map[:, pl.ds(j * cap, cap)] = jnp.where(column == at, 1.0, 0.0).astype(BF16)
 
+    four = n == 4
+    half = ag_chunks // 2
+    step = jnp.where(2 * p < n, 1, -1)
+    inner = (p > 0) & (p < n - 1)
+    way_far = jnp.where(2 * p < n, 0, 1)
+    way_end = 1 - way_far
+
     def z_copy(g, c, way, target):
         piece = gathered.at[g, :, span(c, ag_tile)]
         return pltpu.make_async_remote_copy(
@@ -241,13 +248,22 @@
                 pick_map[...], tokens_all[:, cols], preferred_element_type=F32
             ).astype(BF16)
 
-            @pl.when(p < n - 1)
-            def _():
-                z_copy(p, c, 0, p + 1).start()
-
-            @pl.when(p > 0)
-            def _():
-                z_copy(p, c, 1, p - 1).start()
+            if four:
+                @pl.when(inner)
+                def _():
+                    z_copy(p, c, way_end, p - step).start()
+
+                @pl.when(jnp.logical_not(inner) | (c < half))
+                def _():
+                    z_copy(p, c, way_far, p + step).start()
+            else:
+                @pl.when(p < n - 1)
+                def _():
+                    z_copy(p, c, 0, p + 1).start()
+
+                @pl.when(p > 0)
+                def _():
+                    z_copy(p, c, 1, p - 1).start()
 
     map_rows = min(group, 512) if keep_map else 256
 
@@ -377,41 +393,109 @@
     chance = jnp.sum(jnp.where(mine, jax.nn.sigmoid(logits), 0.0), axis=1, keepdims=True)
     prob[...] = jnp.broadcast_to(chance, prob.shape)
 
-    def side_group(t, side):
-        return p + t * (2 * side - 1)
-
-    @pl.loop(1, n)
-    def _(t):
-        for c in range(ag_chunks):
-            for side in range(2):
-                g = side_group(t, side)
-
-                @pl.when((g >= 0) & (g < n))
-                def _():
-                    z_copy(g, c, 0, p).wait_recv()
-                    onward = p + 1 - 2 * side
-
-                    @pl.when((onward >= 0) & (onward < n))
-                    def _():
-                        z_copy(g, c, side, onward).start()
-
-                    absorb(g, c, side)
-                    if c == ag_chunks - 1:
-                        emit(g)
-
-        @pl.when(t < n - 1)
-        def _():
+    def take(g, c):
+        z_copy(g, c, 0, p).wait_recv()
+
+    if four:
+        @pl.when(jnp.logical_not(inner))
+        def _():
+            @pl.loop(0, n - 1)
+            def _(j):
+                g = p + step * jnp.where(j == 0, 1, n - 1 - (j - 1))
+                for c in range(ag_chunks):
+                    take(g, c)
+                    absorb(g, c, 0)
+                emit(g)
+
+        @pl.when(inner)
+        def _():
+            edge, mate, far = p - step, p + step, p + 2 * step
+            for c in range(ag_chunks):
+                take(edge, c)
+                z_copy(edge, c, way_far, mate).start()
+                if c == ag_chunks - 1:
+                    for k in range(half, ag_chunks):
+                        z_copy(p, k, way_far, mate).start()
+                if c >= half:
+                    take(far, c - half)
+                    z_copy(far, c - half, way_end, edge).start()
+                absorb(edge, c, 0)
+                if c == ag_chunks - 1:
+                    emit(edge)
+                if c >= half:
+                    absorb(far, c - half, 1)
+                else:
+                    take(mate, c)
+                    absorb(mate, c, 2)
+            for c in range(ag_chunks - half, ag_chunks):
+                take(far, c)
+                z_copy(far, c, way_end, edge).start()
+                if c == ag_chunks - 1:
+                    for k in range(half):
+                        z_copy(mate, k, way_end, edge).start()
+                absorb(far, c, 1)
+            emit(far)
+            for c in range(half, ag_chunks):
+                take(mate, c)
+                z_copy(mate, c, way_end, edge).start()
+                absorb(mate, c, 2)
+            emit(mate)
+
             @pl.loop(0, rs_chunks + lag)
             def _(s):
-                flow(t, s)
-
-                @pl.when((t == closing) & (s >= lag))
+                @pl.when(s < rs_chunks)
                 def _():
-                    final(s - lag)
+                    forward(far, s)
+
+                @pl.when(s >= lag)
+                def _():
+                    forward(edge, s - lag)
+    else:
+        def side_group(t, side):
+            return p + t * (2 * side - 1)
+
+        @pl.loop(1, n)
+        def _(t):
+            for c in range(ag_chunks):
+                for side in range(2):
+                    g = side_group(t, side)
+
+                    @pl.when((g >= 0) & (g < n))
+                    def _():
+                        z_copy(g, c, 0, p).wait_recv()
+                        onward = p + 1 - 2 * side
+
+                        @pl.when((onward >= 0) & (onward < n))
+                        def _():
+                            z_copy(g, c, side, onward).start()
+
+                        absorb(g, c, side)
+                        if c == ag_chunks - 1:
+                            emit(g)
+
+            @pl.when(t < n - 1)
+            def _():
+                @pl.loop(0, rs_chunks + lag)
+                def _(s):
+                    flow(t, s)
+
+                    @pl.when((t == closing) & (s >= lag))
+                    def _():
+                        final(s - lag)
 
     @pl.loop(0, ag_chunks)
     def _(c):
         first.finish(c)
+
+        @pl.loop(0, n)
+        def _(g):
+            @pl.when((g <= p) & (p < n - 1))
+            def _():
+                z_copy(g, c, 0, p).wait_send()
+
+            @pl.when((g >= p) & (p > 0))
+            def _():
+                z_copy(g, c, 1, p).wait_send()
 
     def consume(c):
         cols = span(c, rs_tile)
@@ -437,25 +521,36 @@
                 kv_w[:, cols], scaled, (((1,), (1,)), ((), ())), preferred_element_type=F32
             )
 
-    @pl.loop(0, rs_chunks + 3 * depth)
+    at_relay, at_collect, at_consume = depth
+
+    after = lag if four else 0
+
+    @pl.loop(0, rs_chunks + at_consume + after)
     def _(s):
-        flow(n - 1, s)
-
-        @pl.when((s < rs_chunks) & (closing == n - 1))
-        def _():
-            final(s)
-
-        @pl.when((s >= depth) & (s < rs_chunks + depth))
-        def _():
-            second.relay(s - depth)
-
-        @pl.when((s >= 2 * depth) & (s < rs_chunks + 2 * depth))
-        def _():
-            second.collect(s - 2 * depth)
-
-        @pl.when(s >= 3 * depth)
-        def _():
-            consume(s - 3 * depth)
+        if four:
+            @pl.when(inner & (s < rs_chunks))
+            def _():
+                forward(p + step, s)
+        else:
+            flow(n - 1, s)
+
+        c = s - after
+
+        @pl.when((c >= 0) & (c < rs_chunks) & (four | (closing == n - 1)))
+        def _():
+            final(c)
+
+        @pl.when((c >= at_relay) & (c < rs_chunks + at_relay))
+        def _():
+            second.relay(c - at_relay)
+
+        @pl.when((c >= at_collect) & (c < rs_chunks + at_collect))
+        def _():
+            second.collect(c - at_collect)
+
+        @pl.when(c >= at_consume)
+        def _():
+            consume(c - at_consume)
 
     moe_store = pltpu.make_async_copy(tokens_all.at[own], moe_out, out_sem.at[0])
     moe_store.start()
@@ -476,16 +571,6 @@
 
     @pl.loop(0, n)
     def _(g):
-        @pl.loop(0, ag_chunks)
-        def _(c):
-            @pl.when((g <= p) & (p < n - 1))
-            def _():
-                z_copy(g, c, 0, p).wait_send()
-
-            @pl.when((g >= p) & (p > 0))
-            def _():
-                z_copy(g, c, 1, p).wait_send()
-
         @pl.when(g != p)
         def _():
             @pl.loop(0, rs_chunks)
@@ -525,7 +610,7 @@
     ag_routed = 0
     eo_routed = 0
     lag = 2
-    depth = 2
+    depth = (2, 4, 5)
     ff_steps = 1
     emit_group = 4
     keep_map = group * experts * cap * 2 <= 4 * 1024 * 1024
@@ -548,10 +633,10 @@
             pltpu.VMEM((group, width), BF16),
             pltpu.VMEM((n, cap, width), BF16),
             pltpu.VMEM((cap, width // ag_chunks), BF16),
-            pltpu.VMEM((2, cap, ff), F32),
-            pltpu.VMEM((2, cap, ff), F32),
-            pltpu.VMEM((2, cap, 128), F32),
-            pltpu.VMEM((2, cap, 128), F32),
+            pltpu.VMEM((3, cap, ff), F32),
+            pltpu.VMEM((3, cap, ff), F32),
+            pltpu.VMEM((3, cap, 128), F32),
+            pltpu.VMEM((3, cap, 128), F32),
             pltpu.VMEM((cap, ff), BF16),
             pltpu.VMEM((n, cap, width), BF16),
             pltpu.VMEM((n + 1, cap, width), BF16),

time: 95.1 us -> 91.5 us (0.962)
  the two profiles are of different devices: /device:TPU:0 before, /device:TPU:9 now
where the time goes in v3:
time: 91.5 us; the launch traced here: 91.3 us
  Pallas kernels  86.9 us (95%)
  local copies, waits for them, and re-layouts  3.73 us (4%)
    pallas_call x1, Pallas kernels, local(): pl.pallas_call(functools.partial(kernel, n, experts, side_a, side_b, ag_c...  86.9 us
    unnamed x2, local copies, waits for them, and re-layouts  3.73 us

profile of v3, /device:TPU:9, one launch (start us, length us, event | category | flops | bytes accessed | tf_op | source)
XLA Modules:
  0.0 91.3 jit_solution(14028846401545507340)
XLA Ops:
  0.6 86.9 %shard_map.104 = (bf16[64,2048]{1,0:T(8,128)(2,1)}, bf16[768,512]{1,0:T(8,128)(2,1)}) custom-call(bf16[64,2048]{1,0:T(8,128)(2,1)} %tokens_hbm.1, bf16[16,128]{1,0:T(8,128)(2,1)} %bitcast.13, bf16[8,2048]{1,0:T(8,128)(2,1)} %bitcast.12, bf16[1,2048,1280]{2,1,0:T(8,128)(2,1)} %gate_hbm.1, bf16[1,2048,1280]{2,1,0:T(8,128)(2,1)} %up_hbm.1, ...), custom_call_target="tpu_custom_call" | custom-call | tf_op jit(solution)/shard_map/pallas_call | solution.py:620
  87.6 1.7 %copy.13 = bf16[64,2048]{1,0:T(8,128)(2,1)} copy(bf16[64,2048]{1,0:T(8,128)(2,1)} %get-tuple-element.8) | data formatting | bytes 524288
  89.2 2.1 %copy.14 = bf16[512,1,6,2,64]{0,4,3,2,1:T(8,128)(2,1)} copy(bf16[512,1,6,2,64]{0,4,3,2,1:T(8,128)(2,1)} %bitcast.11) | data formatting | bytes 1572864

commit v4 on v3

--- a/solution.py
+++ b/solution.py
@@ -610,7 +610,7 @@
     ag_routed = 0
     eo_routed = 0
     lag = 2
-    depth = (2, 4, 5)
+    depth = (2, 5, 7)
     ff_steps = 1
     emit_group = 4
     keep_map = group * experts * cap * 2 <= 4 * 1024 * 1024

time: 91.5 us -> 91.2 us (level)
  the two profiles are of different devices: /device:TPU:9 before, /device:TPU:8 now
where the time goes in v4:
time: 91.2 us; the launch traced here: 91 us
  Pallas kernels  86.6 us (95%)
  local copies, waits for them, and re-layouts  3.73 us (4%)
    pallas_call x1, Pallas kernels, local(): pl.pallas_call(functools.partial(kernel, n, experts, side_a, side_b, ag_c...  86.6 us
    unnamed x2, local copies, waits for them, and re-layouts  3.73 us

profile of v4, /device:TPU:8, one launch (start us, length us, event | category | flops | bytes accessed | tf_op | source)
XLA Modules:
  0.0 91.0 jit_solution(5560108389985855429)
XLA Ops:
  0.6 86.6 %shard_map.104 = (bf16[64,2048]{1,0:T(8,128)(2,1)}, bf16[768,512]{1,0:T(8,128)(2,1)}) custom-call(bf16[64,2048]{1,0:T(8,128)(2,1)} %tokens_hbm.1, bf16[16,128]{1,0:T(8,128)(2,1)} %bitcast.13, bf16[8,2048]{1,0:T(8,128)(2,1)} %bitcast.12, bf16[1,2048,1280]{2,1,0:T(8,128)(2,1)} %gate_hbm.1, bf16[1,2048,1280]{2,1,0:T(8,128)(2,1)} %up_hbm.1, ...), custom_call_target="tpu_custom_call" | custom-call | tf_op jit(solution)/shard_map/pallas_call | solution.py:620
  87.2 1.7 %copy.13 = bf16[64,2048]{1,0:T(8,128)(2,1)} copy(bf16[64,2048]{1,0:T(8,128)(2,1)} %get-tuple-element.8) | data formatting | bytes 524288
  88.9 2.1 %copy.14 = bf16[512,1,6,2,64]{0,4,3,2,1:T(8,128)(2,1)} copy(bf16[512,1,6,2,64]{0,4,3,2,1:T(8,128)(2,1)} %bitcast.11) | data formatting | bytes 1572864
